TPU v7x, 128 devices: a whole 4x4x4 slice. The times are simulated.
128 devices in a mesh: gx: 16 (over y, x), gy: 8 (over z, core).
Axes of the slice: x: 4, y: 4, z: 4, core: 2. Of those that a mesh axis runs over, the one named last changes fastest.
Arguments:
- basis: float32 [32, 256, 128, 256], P(None, 'gx', 'gy'), may hold values from -0.09375 to 0.09375
- reaction: float32 [256, 128, 256], P('gx', 'gy'), may hold values from 0.5 to 4
Outputs:
- extended: float32 [32, 256, 128, 256], P(None, 'gx', 'gy')
- coarse: float32 [128, 5, 32, 32], replicated
All inputs are finite; a program needn't handle non-finite values.
Results may differ from a plain program's by a relative error of at most 0.000071.
Values sent between devices are 32-bit elements; how exact they have to be, the bound alone decides.
A program may use at most 128 MiB of HBM per device.

v0:
```python
import jax
import jax.numpy as jnp
from jax import lax
from jax.sharding import PartitionSpec as P

SWEEPS = 4


OMEGA = 0.8


def with_halo(shard, sides, width):
    edges = {}
    for axis, dim in sides:
        size, length = (lax.axis_size(axis), shard.shape[dim])
        up = [(i, (i + 1) % size) for i in range(size - 1)]
        last = lax.slice_in_dim(shard, length - width, length, axis=dim)
        first = lax.slice_in_dim(shard, 0, width, axis=dim)
        edges[dim] = (
            lax.ppermute(last, axis, up),
            lax.ppermute(first, axis, [(b, a) for a, b in up]),
        )
    done = []
    for _, dim in sides:
        low, high = edges[dim]
        around = [(width, width) if d in done else (0, 0) for d in range(shard.ndim)]
        shard = jnp.concatenate([jnp.pad(low, around), shard, jnp.pad(high, around)], axis=dim)
        done.append(dim)
    return shard


def stencil(field, coef):
    padded = jnp.pad(field, ((0, 0), (1, 1), (1, 1), (1, 1)))
    beside = padded[:, 2:, 1:-1, 1:-1] + padded[:, :-2, 1:-1, 1:-1]
    beside = beside + padded[:, 1:-1, 2:, 1:-1] + padded[:, 1:-1, :-2, 1:-1]
    beside = beside + padded[:, 1:-1, 1:-1, 2:] + padded[:, 1:-1, 1:-1, :-2]
    return (6.0 + coef) * field - beside


def couple(own, other):
    width = own.shape[0]
    return -jnp.dot(
        own.reshape(width, -1),
        other.reshape(width, -1).T,
        precision=lax.Precision.HIGHEST,
        preferred_element_type=jnp.float32,
    )


def on_device(basis, reaction):
    width, cx, cy, cz = basis.shape
    padded = with_halo(basis, (("gx", 1), ("gy", 2)), 1)
    left_face = padded[:, 0, 1:-1, :]
    right_face = padded[:, -1, 1:-1, :]
    lower_face = padded[:, 1:-1, 0, :]
    upper_face = padded[:, 1:-1, -1, :]
    xpos = lax.broadcasted_iota(jnp.int32, (cx, cy, cz), 0)
    ypos = lax.broadcasted_iota(jnp.int32, (cx, cy, cz), 1)
    inner = (xpos >= 1) & (xpos <= cx - 2) & (ypos >= 1) & (ypos <= cy - 2)
    phi = basis
    for sweep in range(SWEEPS):
        update = OMEGA * stencil(phi, reaction) / (6.0 + reaction)
        phi = phi - jnp.where(inner[None], update, jnp.float32(0.0))
    applied = stencil(phi, reaction)
    diag = jnp.dot(
        phi.reshape(width, -1),
        applied.reshape(width, -1).T,
        precision=lax.Precision.HIGHEST,
        preferred_element_type=jnp.float32,
    )
    blocks = jnp.stack(
        [
            diag,
            couple(basis[:, 0], left_face),
            couple(basis[:, -1], right_face),
            couple(basis[:, :, 0], lower_face),
            couple(basis[:, :, -1], upper_face),
        ]
    )
    coarse = lax.all_gather(blocks[None], ("gx", "gy"), axis=0, tiled=True)
    return (phi, coarse)


def solution(mesh):
    placed = (P(None, "gx", "gy", None), P("gx", "gy", None))
    return jax.shard_map(
        on_device,
        mesh=mesh,
        in_specs=placed,
        out_specs=(P(None, "gx", "gy", None), P()),
        check_vma=False,
    )
```

profile of v0, /device:TPU:1, one launch (start us, length us, event | category | flops | bytes accessed | tf_op | source)
XLA Modules:
  0.0 217.7 jit_solution(16846393999798236059)
XLA Ops:
  7.2 0.0 all-gather.3.cloned.1.call-start
  7.2 0.0 copy-start.1
  7.2 1.4 fusion.77
  8.7 1.1 copy.20
  9.8 4.9 %collective-permute-start = (f32[32,1,16,256]{3,0,2,1:T(8,128)}, f32[32,1,16,256]{3,0,2,1:T(8,128)}, u32[]{:S(2)}, u32[]{:S(2)}) collective-permute-start(f32[32,1,16,256]{3,0,2,1:T(8,128)} %copy.20), channel_id=1, source_target_pairs={{0,8},{8,16},{16,24},{24,32},{32,40},{40,48},{48,56},{56,64},{64,7... | collective-permute-start | bytes 1572872 | tf_op jit(solution)/shard_map/ppermute | solution.py:20
  14.6 1.1 copy.19
  15.8 1.3 collective-permute-start.1
  17.1 4.4 %fusion.76 = (f32[32,16,1,256]{3,2,1,0:T(1,128)S(1)}, f32[32,16,1,256]{3,2,1,0:T(1,128)S(1)}) fusion(f32[32,16,16,256]{3,2,1,0:T(8,128)} %param.2), kind=kLoop, calls=%fused_computation.110 | loop fusion | bytes 2097152 | tf_op jit(solution)/shard_map/slice | solution.py:76
  21.5 1.1 copy.22
  22.6 4.4 %collective-permute-start.2 = (f32[32,16,1,256]{3,0,1,2:T(8,128)}, f32[32,16,1,256]{3,0,1,2:T(8,128)}, u32[]{:S(2)}, u32[]{:S(2)}) collective-permute-start(f32[32,16,1,256]{3,0,1,2:T(8,128)} %copy.22), channel_id=1, source_target_pairs={{0,1},{1,2},{2,3},{3,4},{4,5},{5,6},{6,7},{8,9},{9,10},{10,11},{11... | collective-permute-start | bytes 1572872 | tf_op jit(solution)/shard_map/ppermute | solution.py:20
  27.0 1.1 copy.21
  28.1 2.1 collective-permute-start.3
  30.2 1.0 broadcast_add_fusion
  31.2 0.1 and_and_fusion
  31.3 0.0 copy-done.1
  31.3 9.6 %select_subtract_fusion.3 = f32[32,16,16,256]{3,2,1,0:T(8,128)} fusion(f32[32,16,16,256]{3,2,1,0:T(8,128)S(1)} %copy-done.1, f32[16,16,256]{2,1,0:T(8,128)S(1)} %broadcast_add_fusion, pred[16,16,256]{2,1,0:T(8,128)(4,1)S(1)} %and_and_fusion), kind=kLoop, calls=%fused_computation.74 | loop fusion | flops 23068672 | bytes 17104896 | tf_op jit(solution)/shard_map/sub | solution.py:63
  40.9 21.9 %select_subtract_fusion.2 = f32[32,16,16,256]{3,2,1,0:T(8,128)S(1)} fusion(f32[32,16,16,256]{3,2,1,0:T(8,128)} %select_subtract_fusion.3, f32[16,16,256]{2,1,0:T(8,128)S(1)} %broadcast_add_fusion, pred[16,16,256]{2,1,0:T(8,128)(4,1)S(1)} %and_and_fusion), kind=kLoop, calls=%fused_computation.73 | loop fusion | flops 23068672 | bytes 17104896 | tf_op jit(solution)/shard_map/sub | solution.py:63
  62.8 9.6 %select_subtract_fusion.1 = f32[32,16,16,256]{3,2,1,0:T(8,128)} fusion(f32[32,16,16,256]{3,2,1,0:T(8,128)S(1)} %select_subtract_fusion.2, f32[16,16,256]{2,1,0:T(8,128)S(1)} %broadcast_add_fusion, pred[16,16,256]{2,1,0:T(8,128)(4,1)S(1)} %and_and_fusion), kind=kLoop, calls=%fused_computation.72 | loop fusion | flops 23068672 | bytes 17104896 | tf_op jit(solution)/shard_map/sub | solution.py:63
  72.4 21.9 %select_subtract_fusion = f32[32,16,16,256]{3,2,1,0:T(8,128)S(1)} fusion(f32[32,16,16,256]{3,2,1,0:T(8,128)} %select_subtract_fusion.1, f32[16,16,256]{2,1,0:T(8,128)S(1)} %broadcast_add_fusion, pred[16,16,256]{2,1,0:T(8,128)(4,1)S(1)} %and_and_fusion), kind=kLoop, calls=%fused_computation.71 | loop fusion | flops 23068672 | bytes 17104896 | tf_op jit(solution)/shard_map/sub | solution.py:63
  94.3 0.0 copy-start
  94.3 9.3 %fusion.37 = f32[32,16,16,256]{3,2,1,0:T(8,128)} fusion(f32[32,16,16,256]{3,2,1,0:T(8,128)S(1)} %select_subtract_fusion, f32[16,16,256]{2,1,0:T(8,128)S(1)} %broadcast_add_fusion), kind=kLoop, calls=%fused_computation.67 | loop fusion | flops 14680064 | bytes 17039360 | tf_op jit(solution)/shard_map/sub | solution.py:37
  103.6 0.0 copy-done
  103.6 16.2 %fusion.58 = f32[5,32,32]{2,1,0:T(8,128)S(1)} fusion(f32[32,16,16,256]{3,2,1,0:T(8,128)} %fusion.37, f32[32,16,16,256]{3,2,1,0:T(8,128)S(1)} %select_subtract_fusion), kind=kOutput, calls=%fused_computation.92 | convolution fusion | flops 805306368 | bytes 16793600 | tf_op jit(solution)/shard_map/dot_general | solution.py:65
  119.8 0.0 collective-permute-done
  119.8 1.9 fusion.52
  121.7 0.0 collective-permute-done.1
  121.7 1.9 fusion.49
  123.6 0.0 collective-permute-done.2
  123.6 1.9 fusion.46
  125.5 0.0 collective-permute-done.3
  125.5 0.8 fusion.43
  126.3 0.0 copy-start.2
  126.3 0.6 copy-done.2
  127.0 0.0 all-gather.3.cloned.1.call-update
  127.0 74.6 %all-gather.3.cloned.1.call-done = f32[640,32,32]{2,1,0:T(8,128)} async-done(((f32[5,32,32]{2,1,0:T(8,128)}), f32[640,32,32]{2,1,0:T(8,128)}) %all-gather.3.cloned.1.call-update) | async-done | bytes 2621456 | tf_op jit(solution)/shard_map/all_gather | solution.py:80
  201.6 9.2 %copy.17 = f32[128,5,32,32]{0,3,2,1:T(8,128)} copy(f32[128,5,32,32]{3,2,1,0:T(8,128)} %bitcast.81) | data formatting | bytes 5242880
  (2 shorter events, 0.0 us)
Async XLA Ops:
  7.2 194.4 %all-gather.3.cloned.1.call-start = ((), (), s32[]{:S(2)}) async-start(), calls=%async_computation | async-start | bytes 10567680 | tf_op jit(solution)/shard_map/all_gather | solution.py:80
  7.2 24.1 %copy-start.1 = (f32[32,16,16,256]{3,2,1,0:T(8,128)S(1)}, f32[32,16,16,256]{3,2,1,0:T(8,128)}, u32[]{:S(2)}) copy-start(f32[32,16,16,256]{3,2,1,0:T(8,128)} %param.2) | copy-start | bytes 25165828
  9.8 110.1 %collective-permute-start = (f32[32,1,16,256]{3,0,2,1:T(8,128)}, f32[32,1,16,256]{3,0,2,1:T(8,128)}, u32[]{:S(2)}, u32[]{:S(2)}) collective-permute-start(f32[32,1,16,256]{3,0,2,1:T(8,128)} %copy.20), channel_id=1, source_target_pairs={{0,8},{8,16},{16,24},{24,32},{32,40},{40,48},{48,56},{56,64},{64,7... | collective-permute-start | bytes 1572872 | tf_op jit(solution)/shard_map/ppermute | solution.py:20
  15.8 105.9 %collective-permute-start.1 = (f32[32,1,16,256]{3,0,2,1:T(8,128)}, f32[32,1,16,256]{3,0,2,1:T(8,128)}, u32[]{:S(2)}, u32[]{:S(2)}) collective-permute-start(f32[32,1,16,256]{3,0,2,1:T(8,128)} %copy.19), channel_id=1, source_target_pairs={{8,0},{16,8},{24,16},{32,24},{40,32},{48,40},{56,48},{64,56},{72,6... | collective-permute-start | bytes 1572872 | tf_op jit(solution)/shard_map/ppermute | solution.py:21
  22.6 101.0 %collective-permute-start.2 = (f32[32,16,1,256]{3,0,1,2:T(8,128)}, f32[32,16,1,256]{3,0,1,2:T(8,128)}, u32[]{:S(2)}, u32[]{:S(2)}) collective-permute-start(f32[32,16,1,256]{3,0,1,2:T(8,128)} %copy.22), channel_id=1, source_target_pairs={{0,1},{1,2},{2,3},{3,4},{4,5},{5,6},{6,7},{8,9},{9,10},{10,11},{11... | collective-permute-start | bytes 1572872 | tf_op jit(solution)/shard_map/ppermute | solution.py:20
  28.1 97.4 %collective-permute-start.3 = (f32[32,16,1,256]{3,0,1,2:T(8,128)}, f32[32,16,1,256]{3,0,1,2:T(8,128)S(1)}, u32[]{:S(2)}, u32[]{:S(2)}) collective-permute-start(f32[32,16,1,256]{3,0,1,2:T(8,128)} %copy.21), channel_id=1, source_target_pairs={{1,0},{2,1},{3,2},{4,3},{5,4},{6,5},{7,6},{9,8},{10,9},{11,10},{12... | collective-permute-start | bytes 1572872 | tf_op jit(solution)/shard_map/ppermute | solution.py:21
  94.3 9.3 %copy-start = (f32[32,16,16,256]{3,2,1,0:T(8,128)}, f32[32,16,16,256]{3,2,1,0:T(8,128)S(1)}, u32[]{:S(2)}) copy-start(f32[32,16,16,256]{3,2,1,0:T(8,128)S(1)} %select_subtract_fusion) | copy-start | bytes 25165828
  126.3 0.6 copy-start.2
Sparse Core Ops, SparseCore 0:
  127.1 74.4 all-gather.2
where the time goes:
time: 218 us
  waiting for transfers between devices  74.6 us (34%)
  other arithmetic  73.3 us (34%)
  matrix products  22.7 us (10%)
  local copies, waits for them, and re-layouts  20.2 us (9%)
  between operations  14.2 us (7%)
  starting transfers between devices  12.7 us (6%)
    all_gather x1, waiting for transfers between devices, on_device(): coarse = lax.all_gather(blocks[None], ('gx', 'gy'), axis=0, tiled=True)  74.6 us
    sub x4, other arithmetic, on_device(): phi = phi - jnp.where(inner[None], update, jnp.float32(0.0))  63 us
    dot_general x1, matrix products, on_device(): jnp.dot(phi.reshape(width, -1), applied.reshape(width, -1).T, precision=l...  16.2 us
    unnamed x11, local copies, waits for them, and re-layouts  14.3 us
    sub x1, other arithmetic, stencil(): return (6.0 + coef) * field - beside  9.28 us
    ppermute x2, starting transfers between devices, with_halo(): lax.ppermute(last, axis, up)  9.26 us
    dot_general x4, matrix products, couple(): jnp.dot(own.reshape(width, -1), other.reshape(width, -1).T, precision=lax...  6.45 us
    slice x1, local copies, waits for them, and re-layouts, on_device(): basis[:, :, 0]  4.41 us
  transfers between devices with their start and end apart: 5, of which 1 were waited for; matrix products, arithmetic and copies ran while one was open for 47% of the time, Pallas kernels for 0%

commit v1 on v0

v1 whole, which is shorter than its diff:
```python
import functools

import jax
import jax.numpy as jnp
from jax import lax
from jax.experimental import pallas as pl
from jax.experimental.pallas import tpu as pltpu
from jax.sharding import PartitionSpec as P

MESH = pl.DeviceIdType.MESH
ANY = pl.BlockSpec(memory_space=pl.ANY)
VM = pl.BlockSpec(memory_space=pltpu.VMEM)
OMEGA = 0.8
K, CX, CY, CZ = 32, 16, 16, 256
HALF = CZ // 2
HX = CY // 2
F32, BF16 = jnp.float32, jnp.bfloat16
LAG = 2
EDGES_AT, PARTS_AT, LINE_AT = 12, 14, 16


def split(v):
    hi = v.astype(BF16)
    return hi, (v - hi.astype(F32)).astype(BF16)


def lanes(rows):
    return lax.broadcasted_iota(jnp.int32, (rows, 128), 1)


def split_row(new, zin, slot, y):
    hi, lo = split(new)
    rows = pl.ds((y - 1) * K, K)
    zin[slot, rows, :CZ] = hi
    zin[slot, rows, CZ:] = lo


def sweep_row(src, dst, w, zin, zout, band, x):
    slot = lax.rem(x, 2)
    beside_z = jnp.dot(zin[slot], band[...], preferred_element_type=F32)
    low = src[x, 0]
    dst[x, 0] = low
    mid = src[x, 1]
    for y in range(1, CY - 1):
        high = src[x, y + 1]
        beside = (src[x - 1, y] + src[x + 1, y]) + (low + high)
        beside = beside + beside_z[(y - 1) * K:y * K]
        scaled = beside.reshape(K // 8, 8, CZ) * w[x, y][None]
        new = (1.0 - OMEGA) * mid + scaled.reshape(K, CZ)
        dst[x, y] = new
        if zout is not None:
            split_row(new, zout, slot, y)
        low, mid = mid, high
    dst[x, CY - 1] = mid


def product_row(phi, half, lhs, rhs, x, slot, bottom):
    last = lanes(K) == 127
    mid = phi[x, 0]
    for y in range(CY):
        d0, d1 = pltpu.roll(mid[:, :HALF], 127, 1), pltpu.roll(mid[:, HALF:], 127, 1)
        after = jnp.concatenate([jnp.where(last, d1, d0), jnp.where(last, 0.0, d1)], axis=1)
        out = (mid.reshape(K // 8, 8, CZ) * half[x, y][None]).reshape(K, CZ) - after
        high = None
        if y < CY - 1:
            high = phi[x, y + 1]
            out = out - high
        if not bottom:
            out = out - phi[x + 1, y]
        zs = pl.ds(y * CZ, CZ)
        hi, lo = split(mid)
        lhs[slot, :K, zs] = hi
        lhs[slot, K:, zs] = lo
        hi, lo = split(out)
        rhs[slot, :K, zs] = hi
        rhs[slot, K:, zs] = lo
        mid = high


def product(lhs, rhs):
    return lax.dot_general(lhs, rhs, (((1,), (1,)), ((), ())), preferred_element_type=F32)


def fold(total):
    return (total[:K, :K] + total[K:, K:]) + (total[:K, K:] + total[K:, :K])


def coefficients(reaction, w, half, x):
    for y in range(CY):
        d = 6.0 + reaction[x, pl.ds(y, 1), :]
        w[x, y] = jnp.broadcast_to(OMEGA / d, (8, CZ))
        half[x, y] = jnp.broadcast_to(0.5 * d, (8, CZ))


def pack(v, tall):
    tall[:, 0:K] = v
    out = tall[pl.ds(0, 8, stride=4), :]
    for r in range(1, 4):
        part = pltpu.roll(tall[pl.ds(r, 8, stride=4), :], 32 * r, 1)
        out = jnp.where(lanes(8) >= 32 * r, part, out)
    return out


def edge_product(own, other, count):
    total = jnp.zeros((2 * K, 2 * K), F32)
    for c in range(count):
        total = total + product(jnp.concatenate(split(own(c)), axis=0), jnp.concatenate(split(other(c)), axis=0))
    return -fold(total)


def main_kernel(n_gx, n_gy, basis, reaction, l4, rows, l0, l1, l2, l3, w, half, lhs, rhs, acc, band, z0, z1, z2, z3,
                got_xl, got_xu, got_yl, part, got_part, tall, edge, diag, ge, gd, wide,
                in_sem, face_send, face_recv, part_sem, e_send, e_recv, d_send, d_recv):
    gx, gy = lax.axis_index("gx"), lax.axis_index("gy")
    cx, cy, cz, core = gx % 4, gx // 4, gy // 2, gy % 2
    levels = (l0, l1, l2, l3, l4)
    zins = (z0, z1, z2, z3)
    twin = {"gx": gx, "gy": cz * 2 + (1 - core)}
    up_x, down_x, up_y = {"gx": gx + 1, "gy": gy}, {"gx": gx - 1, "gy": gy}, {"gx": gx, "gy": gy + 1}
    has_lx, has_ux, has_ly, has_uy = gx > 0, gx < n_gx - 1, gy > 0, gy < n_gy - 1
    beyond = {"gx": gx, "gy": lax.rem(gy + 2 * core + n_gy - 1, n_gy)}

    def on_line(n):
        return {"gx": gx, "gy": ((cz + n) % 4) * 2 + core}

    def on_plane(n):
        return {"gx": ((cy + n // 4) % 4) * 4 + (cx + n % 4) % 4, "gy": gy}

    barrier = pltpu.get_barrier_semaphore()

    def greet(device):
        pl.semaphore_signal(barrier, inc=1, device_id=device, device_id_type=MESH)

    for n in range(1, 4):
        greet(on_line(n))

    @pl.loop(1, 16)
    def _(n):
        greet(on_plane(n))

    greet(twin)
    greet(beyond)

    for x in (0, CX - 1, *range(1, CX - 1)):
        for y in range(CY):
            pltpu.make_async_copy(basis.at[:, x, y, :], l0.at[x, y], in_sem.at[x]).start()

    def arrived(x):
        pltpu.make_async_copy(l0.at[x], l0.at[x], in_sem.at[x]).wait()

    def seed(x):
        @pl.loop(0, CY)
        def _(y):
            v = l0[x, y]
            for level in range(1, 5):
                levels[level][x, y] = v

    def split_first(x):
        for y in range(1, CY - 1):
            split_row(l0[x, y], z0, lax.rem(x, 2), y)

    @pl.loop(0, CX)
    def _(x):
        coefficients(reaction, w, half, x)

    to = lax.broadcasted_iota(jnp.int32, (CZ, CZ), 1)
    at = lax.broadcasted_iota(jnp.int32, (CZ, CZ), 0)
    near = jnp.where(jnp.abs(to - at) == 1, 1.0, 0.0).astype(BF16)
    band[:CZ] = near
    band[CZ:] = near
    acc[...] = jnp.zeros_like(acc)
    edge[...] = jnp.zeros_like(edge)

    pl.semaphore_wait(barrier, 20)

    def face(src, dst, which, device):
        return pltpu.make_async_remote_copy(src, dst, face_send.at[which], face_recv.at[which], device_id=device, device_id_type=MESH)

    send_xl = face(l0.at[CX - 1, pl.ds(0, HX)], got_xl, 0, up_x)
    send_xu = face(l0.at[0, pl.ds(HX, HX)], got_xu, 1, down_x)
    send_y = face(l0.at[:, CY - 1], got_yl, 2, up_y)
    send_part = pltpu.make_async_remote_copy(part, got_part, part_sem.at[0], part_sem.at[1], device_id=up_x, device_id_type=MESH)

    arrived(0)
    arrived(CX - 1)

    @pl.when(has_ux)
    def _():
        send_xl.start()

    @pl.when(has_lx)
    def _():
        send_xu.start()

    seed(0)
    seed(CX - 1)
    arrived(1)
    split_first(1)

    def start_y_face():
        for x in range(4, CX - 1):
            arrived(x)

        @pl.when(has_uy)
        def _():
            send_y.start()

    def edges():
        @pl.when(has_ux)
        def _():
            send_xu.wait_recv()
            part[...] = pack(edge_product(lambda c: got_xu[c], lambda c: l0[CX - 1, HX + c], HX), tall)
            send_part.start()

        @pl.when(has_ly)
        def _():
            send_y.wait_recv()
            edge[8:16, :] = pack(edge_product(lambda c: l0[c, 0], lambda c: got_yl[c], CX), tall)

        @pl.when(has_lx)
        def _():
            send_xl.wait_recv()
            edge[0:8, :] = pack(edge_product(lambda c: l0[0, c], lambda c: got_xl[c], HX), tall)

    def remote(src, dst, sems, i, device):
        return pltpu.make_async_remote_copy(src, dst, sems[0].at[i], sems[1].at[i], device_id=device, device_id_type=MESH)

    def line_of(block, all_of, sems):
        height = block.shape[0]
        return lambda n: remote(block, all_of.at[gx, cz, pl.ds(core * height, height)], sems, 0, on_line(n))

    def plane_of(all_of, sems):
        height = all_of.shape[2] // 2
        mine = all_of.at[gx, :, pl.ds(core * height, height)]
        return lambda n: remote(mine, mine, sems, 1, on_plane(n))

    def twin_of(all_of, sems):
        height = all_of.shape[2] // 2
        mine = all_of.at[:, :, pl.ds(core * height, height)]
        return remote(mine, mine, sems, 2, twin)

    def line_start(block, all_of, sems):
        height = block.shape[0]
        for n in range(1, 4):
            line_of(block, all_of, sems)(n).start()
        all_of[gx, cz, pl.ds(pl.multiple_of(core * height, 8), height)] = block[...]

    def line_ref(all_of):
        return all_of.at[0, pl.ds(0, 3), pl.ds(0, all_of.shape[2] // 2)]

    def plane_ref(all_of):
        return all_of.at[pl.ds(0, 15), :, pl.ds(0, all_of.shape[2] // 2)]

    def all_recv(ref, sems, i):
        remote(ref, ref, sems, i, twin).wait_recv()

    def all_sent(ref, sems, i):
        remote(ref, ref, sems, i, twin).wait_send()

    def plane_start(all_of, sems):
        all_recv(line_ref(all_of), sems, 0)

        @pl.loop(1, 16)
        def _(n):
            plane_of(all_of, sems)(n).start()

    es, ds = (e_send, e_recv), (d_send, d_recv)

    def parts():
        @pl.when(has_lx)
        def _():
            send_part.wait_recv()
            edge[0:8, :] += got_part[...]

        line_start(edge, ge, es)

    def spread_edges():
        plane_start(ge, es)

    def step(t, active):
        if 7 in active:
            arrived(t + 1)
        if 6 in active:
            slot = lax.rem(t - 9, 2)
            acc[...] += product(lhs[slot], rhs[slot])
        if 5 in active:
            product_row(l4, half, lhs, rhs, t - 8, lax.rem(t - 8, 2), False)
        for s in (4, 3, 2, 1):
            if s in active:
                sweep_row(levels[s - 1], levels[s], w, zins[s - 1], zins[s] if s < 4 else None, band, t - LAG * (s - 1))
        if 0 in active:
            split_first(t + 1)

    def active_at(t):
        on = []
        if t <= 13:
            on.append(0)
        if t <= 2:
            on.append(7)
        for s in (1, 2, 3, 4):
            if 1 <= t - LAG * (s - 1) <= 14:
                on.append(s)
        if 0 <= t - 8 <= 14:
            on.append(5)
        if 0 <= t - 9 <= 14:
            on.append(6)
        return tuple(on)

    after = {2: start_y_face, EDGES_AT: edges, PARTS_AT: parts, LINE_AT: spread_edges}
    t = 1
    while t <= 23:
        end = t
        while end + 1 <= 23 and active_at(end + 1) == active_at(t) and end not in after:
            end += 1
        on = active_at(t)
        if end == t:
            step(jnp.int32(t), on)
        else:
            lax.fori_loop(t, end + 1, lambda i, c, on=on: (step(i, on), c)[1], 0)
        if end in after:
            after[end]()
        t = end + 1
    product_row(l4, half, lhs, rhs, CX - 1, 1, True)
    total = fold(acc[...] + product(lhs[1], rhs[1]))
    diag[...] = pack(total + total.T, tall)
    line_start(diag, gd, ds)

    all_recv(plane_ref(ge), es, 1)
    twin_of(ge, es).start()
    plane_start(gd, ds)
    twin_of(ge, es).wait_recv()

    flat = ge.reshape(n_gx * n_gy * 16, 128)
    for b, (lower, upper, shift) in enumerate(((1, 2, 128 - n_gy), (3, 4, 127))):
        for q in range(8):
            tile = flat[pl.ds(8 * b + q, 128, stride=16), :].T
            rows[pl.ds(lower * 1024 + q * 128, 128), :] = tile
            for r in range(4):
                wide[b, pl.ds((4 * q + r) * 40, 32), :] = tile[32 * r:32 * r + 32]

        @pl.loop(0, K)
        def _(i):
            for j in range(0, K, 8):
                got = wide[b, pl.ds(j * 40 + i, 8, stride=40), :]
                rows[pl.ds(pl.multiple_of(upper * 1024 + i * K, 8) + j, 8), :] = pltpu.roll(got, shift, 1)

    all_recv(plane_ref(gd), ds, 1)
    twin_of(gd, ds).start()
    twin_of(gd, ds).wait_recv()
    flat_d = gd.reshape(n_gx * n_gy * 8, 128)
    for q in range(8):
        rows[pl.ds(q * 128, 128), :] = flat_d[pl.ds(q, 128, stride=8), :].T

    @pl.when(has_ux)
    def _():
        send_xl.wait_send()
        send_part.wait_send()

    @pl.when(has_lx)
    def _():
        send_xu.wait_send()

    @pl.when(has_uy)
    def _():
        send_y.wait_send()

    for all_of, sems in ((ge, es), (gd, ds)):
        all_sent(line_ref(all_of), sems, 0)
        all_sent(plane_ref(all_of), sems, 1)
        twin_of(all_of, sems).wait_send()


def write_kernel(phi, rows, ext, out, sem, row_sem):
    for x in range(CX):
        for y in range(CY):
            pltpu.make_async_copy(phi.at[x, y], ext.at[:, x, y, :], sem).start()
    pltpu.make_async_copy(rows, out, row_sem).start()
    pltpu.make_async_copy(phi, phi, sem).wait()
    pltpu.make_async_copy(rows, out, row_sem).wait()


def everything(mesh, basis, reaction):
    n_gx, n_gy = mesh.shape["gx"], mesh.shape["gy"]
    n = n_gx * n_gy
    dma = pltpu.SemaphoreType.DMA
    level = pltpu.VMEM((CX, CY, K, CZ), F32)
    coef = pltpu.VMEM((CX, CY, 8, CZ), F32)
    operand = pltpu.VMEM((2, 2 * K, CY * CZ), BF16)
    halves = pltpu.VMEM((2, (CY - 2) * K, 2 * CZ), BF16)
    half_face, face = pltpu.VMEM((HX, K, CZ), F32), pltpu.VMEM((CX, K, CZ), F32)
    small = pltpu.VMEM((8, 128), F32)
    phi, rows = pl.pallas_call(
        functools.partial(main_kernel, n_gx, n_gy),
        out_shape=(pltpu.VMEM((CX, CY, K, CZ), F32), pltpu.VMEM((5 * K * K, n), F32)),
        in_specs=[ANY, VM],
        out_specs=(VM, VM),
        scratch_shapes=[
            level, level, level, level, coef, coef, operand, operand, pltpu.VMEM((2 * K, 2 * K), F32),
            pltpu.VMEM((2 * CZ, CZ), BF16), halves, halves, halves, halves,
            half_face, half_face, face, small, small, pltpu.VMEM((K, 128), F32), pltpu.VMEM((16, 128), F32), small,
            pltpu.VMEM((n_gx, n_gy // 2, 32, 128), F32), pltpu.VMEM((n_gx, n_gy // 2, 16, 128), F32),
            pltpu.VMEM((2, K * 40, 128), F32),
            dma((CX,)), dma((3,)), dma((3,)), dma((2,)), dma((3,)), dma((3,)), dma((3,)), dma((3,)),
        ],
        compiler_params=pltpu.CompilerParams(collective_id=0, has_side_effects=True, vmem_limit_bytes=50 * 1024 * 1024),
        name="everything",
    )(basis, reaction)
    return pl.pallas_call(
        write_kernel,
        out_shape=(jax.ShapeDtypeStruct(basis.shape, F32), jax.ShapeDtypeStruct(rows.shape, F32)),
        in_specs=[VM, VM],
        out_specs=(ANY, ANY),
        scratch_shapes=[dma, dma],
        compiler_params=pltpu.CompilerParams(vmem_limit_bytes=2 * 1024 * 1024),
        name="write",
    )(phi, rows)


def solution(mesh):
    def on_device(basis, reaction):
        extended, rows = everything(mesh, basis, reaction)
        coarse = rows.reshape(5, K, K, rows.shape[1]).transpose(3, 0, 1, 2)
        return extended, coarse

    return jax.shard_map(
        on_device,
        mesh=mesh,
        in_specs=(P(None, "gx", "gy", None), P("gx", "gy", None)),
        out_specs=(P(None, "gx", "gy", None), P()),
        check_vma=False,
    )
```

time: 218 us -> 51.5 us (0.24)
  waiting for transfers between devices: 74.6 us -> 0 us
  other arithmetic: 73.3 us -> 0 us
  Pallas kernels: 0 us -> 50.5 us
  matrix products: 22.7 us -> 0 us
  local copies, waits for them, and re-layouts: 20.2 us -> 0 us
  between operations: 14.2 us -> 0.8 us
  starting transfers between devices: 12.7 us -> 0 us
    all_gather x1 -> x0, waiting for transfers between devices: 74.6 us -> none  [on_device(): coarse = lax.all_gather(blocks[None], ('gx', 'gy'), axis=0, tiled=True)]
    sub x5 -> x0, other arithmetic: 72.2 us -> none  [the longest x4 63 us: on_device(): phi = phi - jnp.where(inner[None], update, jnp.float32(0.0))]
    pallas_call x0 -> x2, Pallas kernels: none -> 50.5 us  [the longest x1 46.5 us: everything(): pl.pallas_call(functools.partial(main_kernel, n_gx, n_gy), out_shape=(plt...]
    dot_general x5 -> x0, matrix products: 22.7 us -> none  [the longest x1 16.2 us: on_device(): jnp.dot(phi.reshape(width, -1), applied.reshape(width, -1).T, precision=l...]
    unnamed x11 -> x0, local copies, waits for them, and re-layouts: 14.3 us -> none
    ppermute x4 -> x0, starting transfers between devices: 12.6 us -> none  [the longest x2 9.26 us: with_halo(): lax.ppermute(last, axis, up)]
    slice x2 -> x0, local copies, waits for them, and re-layouts: 5.84 us -> none  [the longest x1 4.41 us: on_device(): basis[:, :, 0]]
  transfers between devices with their start and end apart: 5 -> 0, of which waited for: 1 -> 0; matrix products, arithmetic and copies ran while one was open for 47% -> 0% of each run, Pallas kernels for 0% -> 0%
where the time goes in v1:
time: 51.5 us; the launch traced here: 51.3 us
  Pallas kernels  50.5 us (98%)
  between operations  0.8 us (2%)
    pallas_call x1, Pallas kernels, everything(): pl.pallas_call(functools.partial(main_kernel, n_gx, n_gy), out_shape=(plt...  46.5 us
    pallas_call x1, Pallas kernels, everything(): pl.pallas_call(write_kernel, out_shape=(jax.ShapeDtypeStruct(basis.shape,...  4.07 us

profile of v1, /device:TPU:1, one launch (start us, length us, event | category | flops | bytes accessed | tf_op | source)
XLA Modules:
  0.0 51.3 jit_solution(9815518677509417157)
XLA Ops:
  0.6 46.5 %everything.1 = (f32[16,16,32,256]{3,2,1,0:T(8,128)S(1)}, f32[5120,128]{1,0:T(8,128)S(1)}) custom-call(f32[32,16,16,256]{3,2,1,0:T(8,128)} %basis.1, f32[16,16,256]{2,1,0:T(8,128)} %reaction.1), custom_call_target="tpu_custom_call" | custom-call | tf_op jit(solution)/shard_map/everything/pallas_call | solution.py:392
  47.1 4.1 %write.1 = (f32[32,16,16,256]{3,2,1,0:T(8,128)}, f32[5120,128]{1,0:T(8,128)}) custom-call(f32[16,16,32,256]{3,2,1,0:T(8,128)S(1)} %get-tuple-element.6.phi, f32[5120,128]{1,0:T(8,128)S(1)} %get-tuple-element.7.rows), custom_call_target="tpu_custom_call" | custom-call | tf_op jit(solution)/shard_map/write/pallas_call | solution.py:408
